TPU v7x, 32 devices: a whole 2x2x4 slice. The times are simulated.
32 devices in a mesh: row: 8 (over y, x, core), col: 4 (over z).
Axes of the slice: x: 2, y: 2, z: 4, core: 2. Of those that a mesh axis runs over, the one named last changes fastest.
Arguments:
- jacobian: float32 [2, 4096, 256], P(None, ('row', 'col')), may hold values from -0.25 to 0.25
Outputs:
- normal_tiles: float32 [8, 2, 4, 512, 512], P('row', None, 'col')
All inputs are finite; a program needn't handle non-finite values.
Results may differ from a plain program's by a relative error of at most 0.0003.
Values sent between devices are 32-bit elements; how exact they have to be, the bound alone decides.
A program may use at most 64 MiB of HBM per device.

v0:
```python
import jax
import jax.numpy as jnp
from jax import lax
from jax.sharding import PartitionSpec as P


def from_partner(block, axis, distance):
    count = lax.axis_size(axis)
    route = []
    for low in range(count):
        high = low | 1 << distance
        if high != low and high < count:
            route += [(low, high), (high, low)]
    return lax.ppermute(block, axis, route)


def partner_rows(block, bit_number):
    return from_partner(block, ("row", "col"), bit_number)


def body(jacobian):
    row_index = lax.axis_index("row")
    col_index = lax.axis_index("col")
    col_count = lax.axis_size("col")
    cycles = lax.axis_size("row") // col_count
    panel_count = jacobian.shape[0]
    width = jacobian.shape[2]
    own_tile = lax.all_gather(jacobian, "col", axis=1, tiled=True)
    tile_size = own_tile.shape[1]
    col_bits = col_count.bit_length() - 1
    low_row = row_index % col_count
    moved = jacobian
    for bit_number in range(col_bits):
        first = partner_rows(moved, bit_number)
        second = partner_rows(first, bit_number + col_bits)
        differ = low_row >> bit_number & 1 != col_index >> bit_number & 1
        moved = jnp.where(differ, second, moved)
    gathered = lax.all_gather(moved, "row", axis=1, tiled=True)
    gathered = gathered.reshape(panel_count, cycles, tile_size, width)
    partners = [gathered[:, turn_index] for turn_index in range(cycles)]

    def product(partner):
        return jnp.einsum("pak,pbk->ab", own_tile, partner, precision=lax.Precision.HIGHEST)

    def empty_tile(partner):
        return jnp.zeros((tile_size, tile_size), jnp.float32)

    results = []
    for turn_index in range(cycles):
        column_tile = col_index + col_count * turn_index
        results.append(
            lax.cond(column_tile <= row_index, product, empty_tile, partners[turn_index])
        )
    blocks = jnp.stack(results, 0)
    return blocks[None, :, None]


def solution(mesh):
    in_specs = (P(None, ("row", "col"), None),)
    out_specs = P("row", None, "col", None, None)
    return jax.shard_map(body, mesh=mesh, in_specs=in_specs, out_specs=out_specs, check_vma=False)
```

profile of v0, /device:TPU:4, one launch (start us, length us, event | category | flops | bytes accessed | tf_op | source)
XLA Modules:
  0.0 115.7 jit_solution(6772489944896085306)
XLA Ops:
  6.5 0.0 all-gather.3.cloned.1.call-start
  6.5 1.6 %collective-permute-start = (f32[2,128,256]{2,1,0:T(8,128)}, f32[2,128,256]{2,1,0:T(8,128)S(1)}, u32[]{:S(2)}, u32[]{:S(2)}) collective-permute-start(f32[2,128,256]{2,1,0:T(8,128)} %param.5), channel_id=1, source_target_pairs={{0,1},{1,0},{2,3},{3,2},{4,5},{5,4},{6,7},{7,6},{8,9},{9,8},{10,11... | collective-permute-start | bytes 786440 | tf_op jit(solution)/shard_map/ppermute | solution.py:14
  8.1 6.7 %collective-permute-done = f32[2,128,256]{2,1,0:T(8,128)S(1)} collective-permute-done((f32[2,128,256]{2,1,0:T(8,128)}, f32[2,128,256]{2,1,0:T(8,128)S(1)}, u32[]{:S(2)}, u32[]{:S(2)}) %collective-permute-start) | collective-permute-done | bytes 262176 | tf_op jit(solution)/shard_map/ppermute | solution.py:14
  14.8 0.0 collective-permute-start.1
  14.8 1.5 %collective-permute-done.1 = f32[2,128,256]{2,1,0:T(8,128)S(1)} collective-permute-done((f32[2,128,256]{2,1,0:T(8,128)S(1)}, f32[2,128,256]{2,1,0:T(8,128)S(1)}, u32[]{:S(2)}, u32[]{:S(2)}) %collective-permute-start.1) | collective-permute-done | bytes 262176 | tf_op jit(solution)/shard_map/ppermute | solution.py:14
  16.3 1.0 broadcast_select_fusion
  17.3 2.7 %collective-permute-start.2 = (f32[2,128,256]{2,1,0:T(8,128)S(1)}, f32[2,128,256]{2,1,0:T(8,128)S(1)}, u32[]{:S(2)}, u32[]{:S(2)}) collective-permute-start(f32[2,128,256]{2,1,0:T(8,128)S(1)} %broadcast_select_fusion), channel_id=1, source_target_pairs={{0,2},{2,0},{1,3},{3,1},{4,6},{6,4},{5,7},{7,5},{8,10},{10,8},{9,1... | collective-permute-start | bytes 786440 | tf_op jit(solution)/shard_map/ppermute | solution.py:14
  20.0 11.3 %collective-permute-done.2 = f32[2,128,256]{2,1,0:T(8,128)S(1)} collective-permute-done((f32[2,128,256]{2,1,0:T(8,128)S(1)}, f32[2,128,256]{2,1,0:T(8,128)S(1)}, u32[]{:S(2)}, u32[]{:S(2)}) %collective-permute-start.2) | collective-permute-done | bytes 262176 | tf_op jit(solution)/shard_map/ppermute | solution.py:14
  31.3 1.5 %collective-permute-start.3 = (f32[2,128,256]{2,1,0:T(8,128)S(1)}, f32[2,128,256]{2,1,0:T(8,128)S(1)}, u32[]{:S(2)}, u32[]{:S(2)}) collective-permute-start(f32[2,128,256]{2,1,0:T(8,128)S(1)} %collective-permute-done.2), channel_id=1, source_target_pairs={{0,8},{8,0},{1,9},{9,1},{2,10},{10,2},{3,11},{11,3},{4,12},{12,4},... | collective-permute-start | bytes 786440 | tf_op jit(solution)/shard_map/ppermute | solution.py:14
  32.8 5.1 %collective-permute-done.3 = f32[2,128,256]{2,1,0:T(8,128)S(1)} collective-permute-done((f32[2,128,256]{2,1,0:T(8,128)S(1)}, f32[2,128,256]{2,1,0:T(8,128)S(1)}, u32[]{:S(2)}, u32[]{:S(2)}) %collective-permute-start.3) | collective-permute-done | bytes 262176 | tf_op jit(solution)/shard_map/ppermute | solution.py:14
  37.8 0.7 broadcast_select_fusion.1
  38.6 0.0 all-gather.3.cloned.1.call-update
  38.6 0.0 all-gather.5.cloned.1.call-start
  38.7 0.7 all-gather.5.cloned.1.call-update
  39.4 30.0 %all-gather.3.cloned.1.call-done = f32[2,1024,256]{2,1,0:T(8,128)} async-done(((f32[2,128,256]{2,1,0:T(8,128)}), f32[2,1024,256]{2,1,0:T(8,128)}) %all-gather.3.cloned.1.call-update) | async-done | bytes 2097168 | tf_op jit(solution)/shard_map/all_gather | solution.py:38
  69.3 1.7 %copy.2 = f32[2,2,512,256]{3,2,0,1:T(8,128)S(1)} copy(f32[2,2,512,256]{3,2,1,0:T(8,128)} %bitcast.17) | data formatting | bytes 4194304 | tf_op jit(solution)/shard_map/cond | solution.py:52
  71.1 27.9 %all-gather.5.cloned.1.call-done = f32[2,512,256]{2,1,0:T(8,128)} async-done(((f32[2,128,256]{2,1,0:T(8,128)}), f32[2,512,256]{2,1,0:T(8,128)}) %all-gather.5.cloned.1.call-update) | async-done | bytes 1048592 | tf_op jit(solution)/shard_map/all_gather | solution.py:28
  99.0 3.1 %conditional.3 = (f32[1,512,512]{2,1,0:T(8,128)S(1)}) conditional(s32[]{:T(128)} %convert_element_type.7, () %tuple.23, (f32[2,2,512,256]{3,2,0,1:T(8,128)S(1)}, f32[2,512,256]{2,1,0:T(8,128)}) %tuple.24), branch_computations={%region_2.3_spmd, %region_3.4_spmd} | conditional | flops 1610612736 | bytes 3145736 | solution.py:52
  99.0 3.1 %convolution_bitcast_fusion.1 = f32[1,512,512]{2,1,0:T(8,128)S(1)} fusion(f32[2,512,256]{2,1,0:T(8,128)} %get-tuple-element.27, f32[2,2,512,256]{3,2,0,1:T(8,128)S(1)} %get-tuple-element.28), kind=kOutput, calls=%fused_computation.3 | convolution fusion | flops 1610612736 | bytes 3145728 | tf_op jit(solution)/shard_map/cond/branch_1_fun/pak,pbk->ab/dot_general | solution.py:43
  102.1 4.1 %conditional.2 = (f32[1,512,512]{2,1,0:T(8,128)}) conditional(s32[]{:T(128)} %convert_element_type.6, () %tuple.21, (f32[2,2,512,256]{3,2,0,1:T(8,128)S(1)}, f32[2,512,256]{2,1,0:T(8,128)}) %tuple.24), branch_computations={%region_0.1_spmd, %region_1.2_spmd} | conditional | flops 1610612736 | bytes 3145736 | solution.py:52
  102.1 4.1 %convolution_bitcast_fusion = f32[1,512,512]{2,1,0:T(8,128)} fusion(f32[2,512,256]{2,1,0:T(8,128)} %get-tuple-element.25, f32[2,2,512,256]{3,2,0,1:T(8,128)S(1)} %get-tuple-element.26), kind=kOutput, calls=%fused_computation | convolution fusion | flops 1610612736 | bytes 3145728 | tf_op jit(solution)/shard_map/cond/branch_1_fun/pak,pbk->ab/dot_general | solution.py:43
  106.2 2.7 %maximum_bitcast_fusion = f32[1,2,1,512,512]{4,3,2,1,0:T(8,128)} fusion(f32[1,512,512]{2,1,0:T(8,128)S(1)} %get-tuple-element.34, f32[1,512,512]{2,1,0:T(8,128)} %get-tuple-element.33), kind=kLoop, calls=%fused_computation.6 | loop fusion | flops 524288 | bytes 4194304 | tf_op jit(solution)/shard_map/broadcast_in_dim | solution.py:55
Async XLA Ops:
  6.5 62.8 %all-gather.3.cloned.1.call-start = ((), (), s32[]{:S(2)}) async-start(), calls=%async_computation | async-start | bytes 2359296 | tf_op jit(solution)/shard_map/all_gather | solution.py:38
  6.5 8.3 %collective-permute-start = (f32[2,128,256]{2,1,0:T(8,128)}, f32[2,128,256]{2,1,0:T(8,128)S(1)}, u32[]{:S(2)}, u32[]{:S(2)}) collective-permute-start(f32[2,128,256]{2,1,0:T(8,128)} %param.5), channel_id=1, source_target_pairs={{0,1},{1,0},{2,3},{3,2},{4,5},{5,4},{6,7},{7,6},{8,9},{9,8},{10,11... | collective-permute-start | bytes 786440 | tf_op jit(solution)/shard_map/ppermute | solution.py:14
  14.8 1.5 %collective-permute-start.1 = (f32[2,128,256]{2,1,0:T(8,128)S(1)}, f32[2,128,256]{2,1,0:T(8,128)S(1)}, u32[]{:S(2)}, u32[]{:S(2)}) collective-permute-start(f32[2,128,256]{2,1,0:T(8,128)S(1)} %collective-permute-done), channel_id=1, source_target_pairs={{0,4},{4,0},{1,5},{5,1},{2,6},{6,2},{3,7},{7,3},{8,12},{12,8},{9,1... | collective-permute-start | bytes 786440 | tf_op jit(solution)/shard_map/ppermute | solution.py:14
  17.3 14.0 %collective-permute-start.2 = (f32[2,128,256]{2,1,0:T(8,128)S(1)}, f32[2,128,256]{2,1,0:T(8,128)S(1)}, u32[]{:S(2)}, u32[]{:S(2)}) collective-permute-start(f32[2,128,256]{2,1,0:T(8,128)S(1)} %broadcast_select_fusion), channel_id=1, source_target_pairs={{0,2},{2,0},{1,3},{3,1},{4,6},{6,4},{5,7},{7,5},{8,10},{10,8},{9,1... | collective-permute-start | bytes 786440 | tf_op jit(solution)/shard_map/ppermute | solution.py:14
  31.3 6.5 %collective-permute-start.3 = (f32[2,128,256]{2,1,0:T(8,128)S(1)}, f32[2,128,256]{2,1,0:T(8,128)S(1)}, u32[]{:S(2)}, u32[]{:S(2)}) collective-permute-start(f32[2,128,256]{2,1,0:T(8,128)S(1)} %collective-permute-done.2), channel_id=1, source_target_pairs={{0,8},{8,0},{1,9},{9,1},{2,10},{10,2},{3,11},{11,3},{4,12},{12,4},... | collective-permute-start | bytes 786440 | tf_op jit(solution)/shard_map/ppermute | solution.py:14
  38.6 60.4 %all-gather.5.cloned.1.call-start = ((), (), s32[]{:S(2)}) async-start(), calls=%async_computation.1 | async-start | bytes 1310720 | tf_op jit(solution)/shard_map/all_gather | solution.py:28
Sparse Core Ops, SparseCore 0:
  38.7 30.5 all-gather.2
  70.9 28.0 all-gather.4
where the time goes:
time: 116 us
  waiting for transfers between devices  83.2 us (72%)
  between operations  13.4 us (12%)
  matrix products  7.14 us (6%)
  starting transfers between devices  5.77 us (5%)
  other arithmetic  4.43 us (4%)
  local copies, waits for them, and re-layouts  1.73 us (1%)
    all_gather x1, waiting for transfers between devices, body(): gathered = lax.all_gather(moved, 'row', axis=1, tiled=True)  30 us
    all_gather x1, waiting for transfers between devices, body(): own_tile = lax.all_gather(jacobian, 'col', axis=1, tiled=True)  27.9 us
    ppermute x4, waiting for transfers between devices, from_partner(): return lax.ppermute(block, axis, route)  24.6 us
    dot_general x2, matrix products, product(): jnp.einsum('pak,pbk->ab', own_tile, partner, precision=lax.Precision.HIGH...  7.14 us
    ppermute x4, starting transfers between devices, from_partner(): return lax.ppermute(block, axis, route)  5.72 us
    broadcast_in_dim x1, other arithmetic, body(): return blocks[None, :, None]  2.71 us
  transfers between devices with their start and end apart: 6, of which 6 were waited for; matrix products, arithmetic and copies ran while one was open for 1% of the time, Pallas kernels for 0%

commit v1 on v0

--- a/solution.py
+++ b/solution.py
@@ -25,7 +25,7 @@
     cycles = lax.axis_size("row") // col_count
     panel_count = jacobian.shape[0]
     width = jacobian.shape[2]
-    own_tile = lax.all_gather(jacobian, "col", axis=1, tiled=True)
+    own_tile = jnp.concatenate(lax.all_gather(jacobian, "col"), axis=1)
     tile_size = own_tile.shape[1]
     col_bits = col_count.bit_length() - 1
     low_row = row_index % col_count

time: 116 us -> 97.8 us (0.84)
  waiting for transfers between devices: 83.2 us -> 67.2 us
  other arithmetic: 4.43 us -> 3.22 us
    all_gather x1, waiting for transfers between devices: 27.9 us -> 0.02 us  [body(): own_tile = jnp.concatenate(lax.all_gather(jacobian, 'col'), axis=1)]
    ppermute x4, waiting for transfers between devices: 24.6 us -> 39 us  [from_partner(): return lax.ppermute(block, axis, route)]
    all_gather x1, waiting for transfers between devices: 30 us -> 27.5 us  [body(): gathered = lax.all_gather(moved, 'row', axis=1, tiled=True)]
    cond x1 -> x0, local copies, waits for them, and re-layouts: 1.73 us -> none  [body(): lax.cond(column_tile <= row_index, product, empty_tile, partners[turn_ind...]
    reshape x0 -> x1, local copies, waits for them, and re-layouts: none -> 1.33 us  [body(): own_tile = jnp.concatenate(lax.all_gather(jacobian, 'col'), axis=1)]
    broadcast_in_dim x1, other arithmetic: 2.71 us -> 1.49 us  [body(): return blocks[None, :, None]]
  transfers between devices with their start and end apart: 6 -> 6, of which waited for: 6 -> 5; matrix products, arithmetic and copies ran while one was open for 1% -> 3% of each run, Pallas kernels for 0% -> 0%
where the time goes in v1:
time: 97.8 us; the launch traced here: 97.2 us
  waiting for transfers between devices  67.2 us (69%)
  between operations  13.4 us (14%)
  matrix products  6.16 us (6%)
  starting transfers between devices  5.84 us (6%)
  other arithmetic  3.22 us (3%)
  local copies, waits for them, and re-layouts  1.33 us (1%)
    ppermute x4, waiting for transfers between devices, from_partner(): return lax.ppermute(block, axis, route)  39 us
    all_gather x1, waiting for transfers between devices, body(): gathered = lax.all_gather(moved, 'row', axis=1, tiled=True)  27.5 us
    dot_general x2, matrix products, product(): jnp.einsum('pak,pbk->ab', own_tile, partner, precision=lax.Precision.HIGH...  6.16 us
    ppermute x4, starting transfers between devices, from_partner(): return lax.ppermute(block, axis, route)  5.8 us
  transfers between devices with their start and end apart: 6, of which 5 were waited for; matrix products, arithmetic and copies ran while one was open for 3% of the time, Pallas kernels for 0%

profile of v1, /device:TPU:4, one launch (start us, length us, event | category | flops | bytes accessed | tf_op | source)
XLA Modules:
  0.0 97.2 jit_solution(4668967928208689086)
XLA Ops:
  6.5 0.0 all-gather.6.cloned.1.call-start
  6.5 0.7 all-gather.6.cloned.1.call-update
  7.3 0.0 all-gather.4.cloned.1.call-start
  7.3 1.6 %collective-permute-start = (f32[2,128,256]{2,1,0:T(8,128)}, f32[2,128,256]{2,1,0:T(8,128)S(1)}, u32[]{:S(2)}, u32[]{:S(2)}) collective-permute-start(f32[2,128,256]{2,1,0:T(8,128)} %param.5), channel_id=1, source_target_pairs={{0,1},{1,0},{2,3},{3,2},{4,5},{5,4},{6,7},{7,6},{8,9},{9,8},{10,11... | collective-permute-start | bytes 786440 | tf_op jit(solution)/shard_map/ppermute | solution.py:14
  8.9 6.7 %collective-permute-done = f32[2,128,256]{2,1,0:T(8,128)S(1)} collective-permute-done((f32[2,128,256]{2,1,0:T(8,128)}, f32[2,128,256]{2,1,0:T(8,128)S(1)}, u32[]{:S(2)}, u32[]{:S(2)}) %collective-permute-start) | collective-permute-done | bytes 262176 | tf_op jit(solution)/shard_map/ppermute | solution.py:14
  15.6 0.0 collective-permute-start.1
  15.6 1.5 %collective-permute-done.1 = f32[2,128,256]{2,1,0:T(8,128)S(1)} collective-permute-done((f32[2,128,256]{2,1,0:T(8,128)S(1)}, f32[2,128,256]{2,1,0:T(8,128)S(1)}, u32[]{:S(2)}, u32[]{:S(2)}) %collective-permute-start.1) | collective-permute-done | bytes 262176 | tf_op jit(solution)/shard_map/ppermute | solution.py:14
  17.2 1.0 %broadcast_select_fusion = f32[2,128,256]{2,1,0:T(8,128)S(1)} fusion(f32[2,128,256]{2,1,0:T(8,128)S(1)} %collective-permute-done.1, f32[2,128,256]{2,1,0:T(8,128)} %param.5, pred[]{:T(512)S(6)} %ne.14), kind=kLoop, calls=%fused_computation.5 | loop fusion | flops 65536 | bytes 786433 | tf_op jit(solution)/shard_map/jit(_where)/select_n | solution.py:37
  18.2 2.7 %collective-permute-start.2 = (f32[2,128,256]{2,1,0:T(8,128)S(1)}, f32[2,128,256]{2,1,0:T(8,128)S(1)}, u32[]{:S(2)}, u32[]{:S(2)}) collective-permute-start(f32[2,128,256]{2,1,0:T(8,128)S(1)} %broadcast_select_fusion), channel_id=1, source_target_pairs={{0,2},{2,0},{1,3},{3,1},{4,6},{6,4},{5,7},{7,5},{8,10},{10,8},{9,1... | collective-permute-start | bytes 786440 | tf_op jit(solution)/shard_map/ppermute | solution.py:14
  20.8 25.9 %collective-permute-done.2 = f32[2,128,256]{2,1,0:T(8,128)S(1)} collective-permute-done((f32[2,128,256]{2,1,0:T(8,128)S(1)}, f32[2,128,256]{2,1,0:T(8,128)S(1)}, u32[]{:S(2)}, u32[]{:S(2)}) %collective-permute-start.2) | collective-permute-done | bytes 262176 | tf_op jit(solution)/shard_map/ppermute | solution.py:14
  46.7 1.5 %collective-permute-start.3 = (f32[2,128,256]{2,1,0:T(8,128)S(1)}, f32[2,128,256]{2,1,0:T(8,128)S(1)}, u32[]{:S(2)}, u32[]{:S(2)}) collective-permute-start(f32[2,128,256]{2,1,0:T(8,128)S(1)} %collective-permute-done.2), channel_id=1, source_target_pairs={{0,8},{8,0},{1,9},{9,1},{2,10},{10,2},{3,11},{11,3},{4,12},{12,4},... | collective-permute-start | bytes 786440 | tf_op jit(solution)/shard_map/ppermute | solution.py:14
  48.2 4.9 %collective-permute-done.3 = f32[2,128,256]{2,1,0:T(8,128)S(1)} collective-permute-done((f32[2,128,256]{2,1,0:T(8,128)S(1)}, f32[2,128,256]{2,1,0:T(8,128)S(1)}, u32[]{:S(2)}, u32[]{:S(2)}) %collective-permute-start.3) | collective-permute-done | bytes 262176 | tf_op jit(solution)/shard_map/ppermute | solution.py:14
  53.1 0.7 broadcast_select_fusion.1
  53.8 0.0 all-gather.4.cloned.1.call-update
  53.8 0.0 all-gather.6.cloned.1.call-done
  53.9 1.3 %copy.6 = f32[2,4,128,256]{3,2,1,0:T(8,128)S(1)} copy(f32[2,4,128,256]{3,2,0,1:T(8,128)} %bitcast.25) | data formatting | bytes 2097152 | tf_op jit(solution)/shard_map/reshape | solution.py:28
  55.2 27.5 %all-gather.4.cloned.1.call-done = f32[2,1024,256]{2,1,0:T(8,128)} async-done(((f32[2,128,256]{2,1,0:T(8,128)}), f32[2,1024,256]{2,1,0:T(8,128)}) %all-gather.4.cloned.1.call-update) | async-done | bytes 2097168 | tf_op jit(solution)/shard_map/all_gather | solution.py:38
  82.7 3.1 %conditional.3 = (f32[1,512,512]{2,1,0:T(8,128)S(1)}) conditional(s32[]{:T(128)} %convert_element_type.7, () %tuple.23, (f32[2,2,512,256]{3,2,1,0:T(8,128)}, f32[2,512,256]{2,1,0:T(8,128)S(1)}) %tuple.38), branch_computations={%region_2.3_spmd, %region_3.4_spmd} | conditional | flops 1610612736 | bytes 3145736 | solution.py:52
  82.7 3.1 %convolution_bitcast_fusion.1 = f32[1,512,512]{2,1,0:T(8,128)S(1)} fusion(f32[2,512,256]{2,1,0:T(8,128)S(1)} %get-tuple-element.27, f32[2,2,512,256]{3,2,1,0:T(8,128)} %get-tuple-element.35), kind=kOutput, calls=%fused_computation.2 | convolution fusion | flops 1610612736 | bytes 3145728 | tf_op jit(solution)/shard_map/cond/branch_1_fun/pak,pbk->ab/dot_general | solution.py:43
  85.8 3.1 %conditional.2 = (f32[1,512,512]{2,1,0:T(8,128)S(1)}) conditional(s32[]{:T(128)} %convert_element_type.6, () %tuple.21, (f32[2,2,512,256]{3,2,1,0:T(8,128)}, f32[2,512,256]{2,1,0:T(8,128)S(1)}) %tuple.39), branch_computations={%region_0.1_spmd, %region_1.2_spmd} | conditional | flops 1610612736 | bytes 3145736 | solution.py:52
  85.8 3.1 %convolution_bitcast_fusion = f32[1,512,512]{2,1,0:T(8,128)S(1)} fusion(f32[2,512,256]{2,1,0:T(8,128)S(1)} %get-tuple-element.25, f32[2,2,512,256]{3,2,1,0:T(8,128)} %get-tuple-element.33), kind=kOutput, calls=%fused_computation | convolution fusion | flops 1610612736 | bytes 3145728 | tf_op jit(solution)/shard_map/cond/branch_1_fun/pak,pbk->ab/dot_general | solution.py:43
  88.9 1.5 %maximum_bitcast_fusion = f32[1,2,1,512,512]{4,3,2,1,0:T(8,128)} fusion(f32[1,512,512]{2,1,0:T(8,128)S(1)} %get-tuple-element.38, f32[1,512,512]{2,1,0:T(8,128)S(1)} %get-tuple-element.37), kind=kLoop, calls=%fused_computation.4 | loop fusion | flops 524288 | bytes 4194304 | tf_op jit(solution)/shard_map/broadcast_in_dim | solution.py:55
Async XLA Ops:
  6.5 47.3 %all-gather.6.cloned.1.call-start = ((), (), s32[]{:S(2)}) async-start(), calls=%async_computation.1 | async-start | bytes 1310720 | tf_op jit(solution)/shard_map/all_gather | solution.py:28
  7.3 75.4 %all-gather.4.cloned.1.call-start = ((), (), s32[]{:S(2)}) async-start(), calls=%async_computation | async-start | bytes 2359296 | tf_op jit(solution)/shard_map/all_gather | solution.py:38
  7.3 8.3 %collective-permute-start = (f32[2,128,256]{2,1,0:T(8,128)}, f32[2,128,256]{2,1,0:T(8,128)S(1)}, u32[]{:S(2)}, u32[]{:S(2)}) collective-permute-start(f32[2,128,256]{2,1,0:T(8,128)} %param.5), channel_id=1, source_target_pairs={{0,1},{1,0},{2,3},{3,2},{4,5},{5,4},{6,7},{7,6},{8,9},{9,8},{10,11... | collective-permute-start | bytes 786440 | tf_op jit(solution)/shard_map/ppermute | solution.py:14
  15.6 1.5 %collective-permute-start.1 = (f32[2,128,256]{2,1,0:T(8,128)S(1)}, f32[2,128,256]{2,1,0:T(8,128)S(1)}, u32[]{:S(2)}, u32[]{:S(2)}) collective-permute-start(f32[2,128,256]{2,1,0:T(8,128)S(1)} %collective-permute-done), channel_id=1, source_target_pairs={{0,4},{4,0},{1,5},{5,1},{2,6},{6,2},{3,7},{7,3},{8,12},{12,8},{9,1... | collective-permute-start | bytes 786440 | tf_op jit(solution)/shard_map/ppermute | solution.py:14
  18.2 28.5 %collective-permute-start.2 = (f32[2,128,256]{2,1,0:T(8,128)S(1)}, f32[2,128,256]{2,1,0:T(8,128)S(1)}, u32[]{:S(2)}, u32[]{:S(2)}) collective-permute-start(f32[2,128,256]{2,1,0:T(8,128)S(1)} %broadcast_select_fusion), channel_id=1, source_target_pairs={{0,2},{2,0},{1,3},{3,1},{4,6},{6,4},{5,7},{7,5},{8,10},{10,8},{9,1... | collective-permute-start | bytes 786440 | tf_op jit(solution)/shard_map/ppermute | solution.py:14
  46.7 6.4 %collective-permute-start.3 = (f32[2,128,256]{2,1,0:T(8,128)S(1)}, f32[2,128,256]{2,1,0:T(8,128)S(1)}, u32[]{:S(2)}, u32[]{:S(2)}) collective-permute-start(f32[2,128,256]{2,1,0:T(8,128)S(1)} %collective-permute-done.2), channel_id=1, source_target_pairs={{0,8},{8,0},{1,9},{9,1},{2,10},{10,2},{3,11},{11,3},{4,12},{12,4},... | collective-permute-start | bytes 786440 | tf_op jit(solution)/shard_map/ppermute | solution.py:14
Sparse Core Ops, SparseCore 0:
  8.9 40.4 all-gather.5
  53.9 28.7 all-gather.3
